TPU v7x, 32 devices: a whole 2x2x4 slice. The times are simulated.
32 devices in a mesh: seq: 8 (over z, x), head: 4 (over y, core).
Axes of the slice: x: 2, y: 2, z: 4, core: 2. Of those that a mesh axis runs over, the one named last changes fastest.
Arguments:
- queries: bfloat16 [8192, 2048], P('seq', 'head'), may hold values from -64 to 64
- keys: bfloat16 [8192, 2048], P('seq', 'head'), may hold values from -16 to 16
- values: bfloat16 [8192, 2048], P('seq', 'head'), may hold values from -6 to 6
- span_bounds: int32 [16, 2], replicated, may hold values from 0 to 8192, as said below
- mem_decay: float32 [8, 16], P(None, 'head'), may hold values from 0.01 to 1
- mem_gate: float32 [16], P('head'), may hold values from -2 to 2
- out_weight: bfloat16 [2048, 4096], P('head'), may hold values from -0.125 to 0.125
Outputs:
- mixed: bfloat16 [8192, 4096], P('seq', 'head')
Inputs may be any that keep to these rules, and one draw needn't show every extreme that they name: `span_bounds`: slot k lies in segment k // 2, inside the k % 2-th of 2 equal parts of it; start <= end, an empty slot has start == end; some slot covers a whole part.
All inputs are finite; a program needn't handle non-finite values.
Results may differ from a plain program's by a relative error of at most 0.0052.
The roundings to bfloat16 on the way count: a program that leaves them out, or rounds other values in their place, can miss the bound.
Values may be sent and summed in bfloat16 or wider, within the bound.
No kernel may reach another device: no remote copies, remote signals or barrier semaphores. Data moves between devices by JAX's collectives and lax.ppermute only.
A program may use at most 128 MiB of HBM per device.

v0:
```python
import math
import jax
import jax.numpy as jnp
from jax import lax
from jax.sharding import PartitionSpec as P

BAND = 512
SPAN_DEV = 2
HIGHEST_PRECISION = lax.Precision.HIGHEST


def from_behind(block, axis, distance):
    devices = range(lax.axis_size(axis))
    route = [(i - distance, i) for i in devices if i - distance in devices]
    return lax.ppermute(block, axis, route)


def feature_map(values_in):
    return jnp.where(values_in > 0, values_in + 1.0, jnp.exp(jnp.minimum(values_in, 0.0)))


def local_attention(
    queries_3d, band_keys, band_values, query_labels, key_labels, shard_index, band_width
):
    seg_rows, head_count, head_width = queries_3d.shape
    block_rows = min(seg_rows, 512)
    key_count = band_keys.shape[0]
    key_pos = jnp.arange(key_count) - band_width
    key_valid = (key_pos >= 0) | (shard_index > 0)
    score_scale = 1.0 / math.sqrt(head_width)

    def attend_block(block_index):
        row_start = block_index * block_rows
        query_block = lax.dynamic_slice_in_dim(queries_3d, row_start, block_rows, 0)
        label_block = lax.dynamic_slice_in_dim(query_labels, row_start, block_rows, 0)
        query_pos = row_start + jnp.arange(block_rows)
        scores = (
            jnp.einsum("qhd,khd->hqk", query_block, band_keys, preferred_element_type=jnp.float32)
            * score_scale
        )
        nearby = (
            (key_pos[None, :] <= query_pos[:, None])
            & (key_pos[None, :] > query_pos[:, None] - band_width)
            & key_valid[None, :]
        )
        same_span = (label_block[:, None] > 0) & (label_block[:, None] == key_labels[None, :])
        visible = nearby | same_span
        scores = jnp.where(visible[None], scores, -1e30)
        top_score = jnp.max(scores, axis=-1, keepdims=True)
        weights = jnp.exp(scores - top_score)
        totals = jnp.sum(weights, axis=-1)
        mixed_out = jnp.einsum(
            "hqk,khd->qhd",
            weights.astype(jnp.bfloat16),
            band_values,
            preferred_element_type=jnp.float32,
        )
        return mixed_out / jnp.transpose(totals)[:, :, None]

    blocks = lax.map(attend_block, jnp.arange(seg_rows // block_rows))
    return blocks.reshape(seg_rows, head_count, head_width)


def body(queries, keys, values, span_bounds, mem_decay, mem_gate, out_weight):
    seg_rows = queries.shape[0]
    head_count = mem_gate.shape[0]
    head_width = queries.shape[1] // head_count
    band_width = BAND
    shard_index = lax.axis_index("seq")
    prev_keys, prev_values = from_behind(
        (keys[seg_rows - band_width :], values[seg_rows - band_width :]), "seq", 1
    )
    key_feats = feature_map(keys.astype(jnp.float32)).reshape(seg_rows, head_count, head_width)
    value_rows = values.astype(jnp.float32).reshape(seg_rows, head_count, head_width)
    state = jnp.einsum("thd,the->hde", key_feats, value_rows, precision=HIGHEST_PRECISION)
    feat_sum = jnp.sum(key_feats, axis=0)
    cumulative = jnp.cumsum(jnp.log(mem_decay), axis=0)
    before = lax.dynamic_index_in_dim(
        cumulative, jnp.maximum(shard_index - 1, 0), 0, keepdims=False
    )
    part_state = lax.all_gather(state[None], "seq", axis=0, tiled=True)
    part_sum = lax.all_gather(feat_sum[None], "seq", axis=0, tiled=True)
    piece_count = part_state.shape[0]
    piece_index = jnp.arange(piece_count)
    factor = jnp.where(
        (piece_index < shard_index)[:, None],
        jnp.exp(jnp.minimum(before[None, :] - cumulative, 0.0)),
        0.0,
    )
    memory = jnp.einsum("nh,nhde->hde", factor, part_state, precision=HIGHEST_PRECISION)
    feat_total = jnp.einsum("nh,nhd->hd", factor, part_sum, precision=HIGHEST_PRECISION)
    query_feats = feature_map(queries.astype(jnp.float32)).reshape(seg_rows, head_count, head_width)
    numer = jnp.einsum("thd,hde->the", query_feats, memory, precision=HIGHEST_PRECISION)
    denom = jnp.einsum("thd,hd->th", query_feats, feat_total, precision=HIGHEST_PRECISION) + 1.0
    readout = numer / denom[:, :, None]
    own_spans = lax.dynamic_slice_in_dim(span_bounds, shard_index * SPAN_DEV, SPAN_DEV, 0)
    positions = shard_index * seg_rows + jnp.arange(seg_rows)
    inside = (positions[:, None] >= own_spans[None, :, 0]) & (
        positions[:, None] < own_spans[None, :, 1]
    )
    slot_ids = (jnp.arange(SPAN_DEV) + 1)[None, :]
    query_labels = jnp.sum(inside.astype(jnp.int32) * slot_ids, axis=1)
    key_labels = jnp.concatenate([jnp.zeros((band_width,), jnp.int32), query_labels])
    band_keys = jnp.concatenate([prev_keys, keys], axis=0).reshape(
        band_width + seg_rows, head_count, head_width
    )
    band_values = jnp.concatenate([prev_values, values], axis=0).reshape(
        band_width + seg_rows, head_count, head_width
    )
    queries_3d = queries.reshape(seg_rows, head_count, head_width)
    local = local_attention(
        queries_3d, band_keys, band_values, query_labels, key_labels, shard_index, band_width
    )
    gate = jax.nn.sigmoid(mem_gate)[None, :, None]
    attended = (
        (gate * readout + (1.0 - gate) * local)
        .astype(jnp.bfloat16)
        .reshape(seg_rows, head_count * head_width)
    )
    gathered = lax.all_gather(attended, "head", axis=1, tiled=True)
    columns = lax.all_to_all(out_weight, "head", split_axis=1, concat_axis=0, tiled=True)
    mixed = jnp.dot(gathered, columns, preferred_element_type=jnp.float32)
    return mixed.astype(jnp.bfloat16)


def solution(mesh):
    return jax.shard_map(
        body,
        mesh=mesh,
        in_specs=(
            P("seq", "head"),
            P("seq", "head"),
            P("seq", "head"),
            P(),
            P(None, "head"),
            P("head"),
            P("head", None),
        ),
        out_specs=P("seq", "head"),
        check_vma=False,
    )
```

profile of v0, /device:TPU:0, one launch (start us, length us, event | category | flops | bytes accessed | tf_op | source)
XLA Modules:
  0.0 270.6 jit_solution(7278276117064473592)
XLA Ops:
  6.5 0.0 copy-start
  6.5 0.0 all-gather.6.cloned.1.call-start
  6.5 1.6 copy.56
  8.1 0.0 copy-start.4
  8.1 0.9 slice.16
  9.0 5.7 %collective-permute-start = (bf16[512,512]{0,1:T(8,128)(2,1)}, bf16[512,512]{0,1:T(8,128)(2,1)}, u32[]{:S(2)}, u32[]{:S(2)}) collective-permute-start(bf16[512,512]{0,1:T(8,128)(2,1)} %slice.16), channel_id=1, source_target_pairs={{0,4},{4,8},{8,12},{12,16},{16,20},{20,24},{24,28},{1,5},{5,9},{9,... | collective-permute-start | bytes 1572872 | tf_op jit(solution)/shard_map/ppermute | solution.py:15
  14.7 0.0 copy-done.6
  14.7 0.5 copy.58
  15.3 0.8 slice.17
  16.1 0.0 copy-done.4
  16.1 3.5 %collective-permute-start.1 = (bf16[512,512]{0,1:T(8,128)(2,1)}, bf16[512,512]{0,1:T(8,128)(2,1)}, u32[]{:S(2)}, u32[]{:S(2)}) collective-permute-start(bf16[512,512]{0,1:T(8,128)(2,1)} %slice.17), channel_id=1, source_target_pairs={{0,4},{4,8},{8,12},{12,16},{16,20},{20,24},{24,28},{1,5},{5,9},{9,... | collective-permute-start | bytes 1572872 | tf_op jit(solution)/shard_map/ppermute | solution.py:15
  19.6 1.8 fusion.35
  21.4 1.8 copy.75
  23.2 3.8 %fusion.29 = f32[4,128,128]{2,1,0:T(8,128)} fusion(f32[1024,4,128]{0,2,1:T(8,128)} %bitcast.87, bf16[1024,512]{1,0:T(8,128)(2,1)} %param.11), kind=kOutput, calls=%fused_computation.42 | convolution fusion | flops 805306368 | bytes 3407872 | tf_op jit(solution)/shard_map/thd,the->hde/dot_general | solution.py:75
  26.9 0.0 all-gather.6.cloned.1.call-update
  27.0 0.0 all-gather.4.cloned.1.call-start
  27.0 0.0 copy-done
  27.1 0.1 constant_dynamic-slice_fusion
  27.1 0.0 copy-done.7
  27.1 37.5 %all_gather.10 = f32[8,4,128]{2,1,0:T(4,128)S(1)} all-gather(f32[1,4,128]{2,1,0:T(4,128)S(1)} %bitcast.97), channel_id=1, replica_groups=mesh['seq'=8,'head'=4] {'seq'}, dimensions={0}, use_global_device_ids=true | all-gather | bytes 18432 | tf_op jit(solution)/shard_map/all_gather | solution.py:82
  64.7 0.0 copy-done.5
  64.7 1.8 fusion.22
  66.5 1.9 copy.81
  68.4 0.0 copy-start.2
  68.4 0.0 copy-start.8
  68.4 0.2 reduce_window_sum.11
  68.6 0.2 dynamic-slice_reduce_fusion
  68.8 0.1 exponential_select_fusion
  68.9 0.2 convolution_bitcast_fusion
  69.0 1.1 fusion.36
  70.1 0.1 fusion.34
  70.3 2.3 copy.55
  72.6 0.0 collective-permute-done
  72.6 2.6 pad_maximum_fusion
  75.2 1.9 copy.61
  77.2 0.0 collective-permute-done.1
  77.2 2.3 pad_maximum_fusion.1
  79.5 2.6 copy.62
  82.1 77.2 %while.14 = (s32[]{:T(128)}, f32[2,512,4,128]{1,0,3,2:T(2,128)}, s32[2]{0:T(128)S(1)}, s32[1024]{0:T(1024)S(1)}, s32[1536]{0:T(1024)S(1)}, /*index=5*/bf16[1024,...) while((s32[]{:T(128)}, f32[2,512,4,128]{1,0,3,2:T(2,128)}, ...), condition=%wide.region_6.7_spmd.clone.clone, body=%wide.region_3.6_spmd.clone.clone.sunk | while | flops 1650986496 | bytes 49885384 | solution.py:60
  82.1 0.6 dynamic_slice.46
  83.3 0.1 broadcast_compare_fusion.2
  83.4 1.4 and_or_fusion.2
  84.9 4.1 %fusion.57 = (f32[4,512]{1,0:T(4,128)S(1)}, f32[4,512,1536]{2,1,0:T(8,128)S(1)}) fusion(pred[512,1536]{1,0:T(8,128)(4,1)S(1)} %and_or_fusion.2, bf16[1536,4,128]{2,0,1:T(8,128)(2,1)S(1)} %get-tuple-element.345, bf16[1024,4,128]{0,2,1:T(8,128)(2,1)} %get-tuple-element.344, s32[]{:T(128)S(6)} %select_n.64), kind=kOutput, calls=%fused_computation.4.clone.1 | convolution fusion | flops 814741504 | bytes 15474692 | tf_op jit(solution)/shard_map/while/body/eval_jaxpr/qhd,khd->hqk/dot_general | solution.py:38
  89.0 3.6 %fusion.58 = f32[4,512]{1,0:T(4,128)S(1)} fusion(f32[4,512,1536]{2,1,0:T(8,128)S(1)} %get-tuple-element.311, f32[4,512]{1,0:T(4,128)S(1)} %get-tuple-element.312, pred[512,1536]{1,0:T(8,128)(4,1)S(1)} %and_or_fusion.2), kind=kLoop, calls=%fused_computation.5.clone.1 | loop fusion | flops 12580864 | bytes 13385728 | tf_op jit(solution)/shard_map/while/body/eval_jaxpr/reduce_sum | solution.py:51
  92.7 6.0 %divide_bitcast_fusion.2 = f32[1,512,4,128]{3,1,2,0:T(8,128)} fusion(bf16[1536,4,128]{2,0,1:T(8,128)(2,1)} %get-tuple-element.346, f32[4,512,1536]{2,1,0:T(8,128)S(1)} %get-tuple-element.311, f32[4,512]{1,0:T(4,128)S(1)} %get-tuple-element.312, pred[512,1536]{1,0:T(8,128)(4,1)S(1)} %and_or_fusion.2, f32[512,4]{0,1:T(4,128)S(1)} %bitcast.94), kind=kOutput, calls=%fused_computation.11.clone.1 | convolution fusion | flops 818151424 | bytes 16007168 | tf_op jit(solution)/shard_map/while/body/eval_jaxpr/hqk,khd->qhd/dot_general | solution.py:52
  98.7 2.4 copy.93
  101.1 19.6 %dynamic_update_slice.10 = f32[2,512,4,128]{1,0,3,2:T(2,128)} dynamic-update-slice(f32[2,512,4,128]{1,0,3,2:T(2,128)} %get-tuple-element.327, f32[1,512,4,128]{1,0,3,2:T(1,128)S(1)} %copy.93, s32[]{:T(128)} %get-tuple-element.326, s32[]{:T(128)} %constant.90.clone.1..sunk, s32[]{:T(128)} %constant.90.clone.1..sunk, s32[]{:T(128)} %constant.90.clone.1..sunk) | dynamic-update-slice | bytes 2097156 | tf_op jit(solution)/shard_map/while/body/jit(dynamic_update_index_in_dim)/dynamic_update_slice | solution.py:60
  120.7 0.6 dynamic_slice.46
  121.9 0.1 broadcast_compare_fusion.2
  122.0 1.4 and_or_fusion.2
  123.5 4.1 %fusion.57 = (f32[4,512]{1,0:T(4,128)S(1)}, f32[4,512,1536]{2,1,0:T(8,128)S(1)}) fusion(pred[512,1536]{1,0:T(8,128)(4,1)S(1)} %and_or_fusion.2, bf16[1536,4,128]{2,0,1:T(8,128)(2,1)S(1)} %get-tuple-element.345, bf16[1024,4,128]{0,2,1:T(8,128)(2,1)} %get-tuple-element.344, s32[]{:T(128)S(6)} %select_n.64), kind=kOutput, calls=%fused_computation.4.clone.1 | convolution fusion | flops 814741504 | bytes 15474692 | tf_op jit(solution)/shard_map/while/body/eval_jaxpr/qhd,khd->hqk/dot_general | solution.py:38
  127.6 3.6 %fusion.58 = f32[4,512]{1,0:T(4,128)S(1)} fusion(f32[4,512,1536]{2,1,0:T(8,128)S(1)} %get-tuple-element.311, f32[4,512]{1,0:T(4,128)S(1)} %get-tuple-element.312, pred[512,1536]{1,0:T(8,128)(4,1)S(1)} %and_or_fusion.2), kind=kLoop, calls=%fused_computation.5.clone.1 | loop fusion | flops 12580864 | bytes 13385728 | tf_op jit(solution)/shard_map/while/body/eval_jaxpr/reduce_sum | solution.py:51
  131.3 6.0 %divide_bitcast_fusion.2 = f32[1,512,4,128]{3,1,2,0:T(8,128)} fusion(bf16[1536,4,128]{2,0,1:T(8,128)(2,1)} %get-tuple-element.346, f32[4,512,1536]{2,1,0:T(8,128)S(1)} %get-tuple-element.311, f32[4,512]{1,0:T(4,128)S(1)} %get-tuple-element.312, pred[512,1536]{1,0:T(8,128)(4,1)S(1)} %and_or_fusion.2, f32[512,4]{0,1:T(4,128)S(1)} %bitcast.94), kind=kOutput, calls=%fused_computation.11.clone.1 | convolution fusion | flops 818151424 | bytes 16007168 | tf_op jit(solution)/shard_map/while/body/eval_jaxpr/hqk,khd->qhd/dot_general | solution.py:52
  137.3 2.4 copy.93
  139.7 19.6 %dynamic_update_slice.10 = f32[2,512,4,128]{1,0,3,2:T(2,128)} dynamic-update-slice(f32[2,512,4,128]{1,0,3,2:T(2,128)} %get-tuple-element.327, f32[1,512,4,128]{1,0,3,2:T(1,128)S(1)} %copy.93, s32[]{:T(128)} %get-tuple-element.326, s32[]{:T(128)} %constant.90.clone.1..sunk, s32[]{:T(128)} %constant.90.clone.1..sunk, s32[]{:T(128)} %constant.90.clone.1..sunk) | dynamic-update-slice | bytes 2097156 | tf_op jit(solution)/shard_map/while/body/jit(dynamic_update_index_in_dim)/dynamic_update_slice | solution.py:60
  159.3 4.0 %reshape.179 = f32[1024,4,128]{0,2,1:T(8,128)} reshape(f32[2,512,4,128]{1,0,3,2:T(2,128)} %get-tuple-element.133) | data formatting | bytes 4194304 | tf_op jit(solution)/shard_map/reshape | solution.py:61
  163.3 4.6 %fusion.27 = f32[4,1,128,128]{3,1,2,0:T(1,128)S(1)} fusion(f32[8,4,1,1]{0,2,3,1:T(1,128)S(1)} %bitcast.96, f32[8,4,128,128]{3,2,1,0:T(8,128)} %bitcast.91), kind=kOutput, calls=%fused_computation.36 | convolution fusion | flops 6291456 | bytes 2359424 | tf_op jit(solution)/shard_map/nh,nhde->hde/dot_general | solution.py:90
  167.9 4.8 %fusion.26 = bf16[1024,4,128]{0,2,1:T(8,128)(2,1)} fusion(f32[1024,4,128]{0,2,1:T(8,128)} %reshape.179, f32[4,128,128]{2,1,0:T(8,128)S(1)} %bitcast.93, f32[1024,4,128]{0,2,1:T(8,128)S(1)} %bitcast.86, f32[4]{0:T(128)S(1)} %get-tuple-element.236, f32[1024,4]{0,1:T(4,128)S(1)} %fusion.32, f32[4]{0:T(128)S(1)} %get-tuple-element.237), kind=kOutput, calls=%fused_computation.35 | convolution fusion | flops 807927808 | bytes 5521440 | tf_op jit(solution)/shard_map/thd,hde->the/dot_general | solution.py:93
  172.7 0.0 all-gather.4.cloned.1.call-update
  172.7 6.6 %copy.64 = bf16[512,4096]{0,1:T(8,128)(2,1)} copy(bf16[512,4096]{1,0:T(8,128)(2,1)} %param.15) | data formatting | bytes 8388608 | tf_op args[6]
  179.3 68.7 %all_to_all.19 = bf16[512,4,1024]{0,2,1:T(8,128)(2,1)} all-to-all(bf16[512,4,1024]{0,2,1:T(8,128)(2,1)} %bitcast.84), channel_id=1, replica_groups=mesh['seq'=8,'head'=4] {'head'}, dimensions={1} | all-to-all | bytes 8388608 | tf_op jit(solution)/shard_map/all_to_all | solution.py:121
  248.0 6.3 %copy.65 = bf16[4,512,1024]{2,1,0:T(8,128)(2,1)} copy(bf16[4,512,1024]{1,2,0:T(8,128)(2,1)} %bitcast.83) | data formatting | bytes 8388608 | tf_op jit(solution)/shard_map/all_to_all | solution.py:121
  254.3 9.4 %convolution_convert_fusion = bf16[1024,1024]{1,0:T(8,128)(2,1)} fusion(bf16[1024,2048]{0,1:T(8,128)(2,1)} %all-gather.4.cloned.1.call-done, bf16[2048,1024]{1,0:T(8,128)(2,1)} %bitcast.90), kind=kOutput, calls=%fused_computation.38 | convolution fusion | flops 4296015872 | bytes 10485760 | tf_op jit(solution)/shard_map/dot_general | solution.py:122
  263.7 0.0 copy-done.1
  (26 shorter events, 0.1 us)
Async XLA Ops:
  6.5 20.5 %copy-start = (s32[16,2]{0,1:T(2,128)S(1)}, s32[16,2]{0,1:T(2,128)}, u32[]{:S(2)}) copy-start(s32[16,2]{0,1:T(2,128)} %param.12) | copy-start | bytes 388
  6.5 8.2 %copy-start.6 = (bf16[1024,512]{1,0:T(8,128)(2,1)S(1)}, bf16[1024,512]{1,0:T(8,128)(2,1)}, u32[]{:S(2)}) copy-start(bf16[1024,512]{1,0:T(8,128)(2,1)} %param.11) | copy-start | bytes 3145732
  6.5 156.8 %all-gather.6.cloned.1.call-start = ((), (), s32[]{:S(2)}) async-start(), calls=%async_computation.2 | async-start | bytes 2359296 | tf_op jit(solution)/shard_map/all_gather | solution.py:81
  8.1 8.0 %copy-start.4 = (bf16[1024,512]{0,1:T(8,128)(2,1)}, bf16[1024,512]{0,1:T(8,128)(2,1)S(1)}, u32[]{:S(2)}) copy-start(bf16[1024,512]{0,1:T(8,128)(2,1)S(1)} %copy.56) | copy-start | bytes 3145732
  9.0 63.6 %collective-permute-start = (bf16[512,512]{0,1:T(8,128)(2,1)}, bf16[512,512]{0,1:T(8,128)(2,1)}, u32[]{:S(2)}, u32[]{:S(2)}) collective-permute-start(bf16[512,512]{0,1:T(8,128)(2,1)} %slice.16), channel_id=1, source_target_pairs={{0,4},{4,8},{8,12},{12,16},{16,20},{20,24},{24,28},{1,5},{5,9},{9,... | collective-permute-start | bytes 1572872 | tf_op jit(solution)/shard_map/ppermute | solution.py:15
  16.1 61.0 %collective-permute-start.1 = (bf16[512,512]{0,1:T(8,128)(2,1)}, bf16[512,512]{0,1:T(8,128)(2,1)}, u32[]{:S(2)}, u32[]{:S(2)}) collective-permute-start(bf16[512,512]{0,1:T(8,128)(2,1)} %slice.17), channel_id=1, source_target_pairs={{0,4},{4,8},{8,12},{12,16},{16,20},{20,24},{24,28},{1,5},{5,9},{9,... | collective-permute-start | bytes 1572872 | tf_op jit(solution)/shard_map/ppermute | solution.py:15
  23.2 4.0 %copy-start.7 = (f32[8,4]{0,1:T(4,128)S(1)}, f32[8,4]{0,1:T(4,128)}, u32[]{:S(2)}) copy-start(f32[8,4]{0,1:T(4,128)} %param.13) | copy-start | bytes 388
  23.2 41.5 %copy-start.5 = (bf16[1024,512]{1,0:T(8,128)(2,1)S(1)}, bf16[1024,512]{1,0:T(8,128)(2,1)}, u32[]{:S(2)}) copy-start(bf16[1024,512]{1,0:T(8,128)(2,1)} %param.9) | copy-start | bytes 3145732
  27.0 227.4 %all-gather.4.cloned.1.call-start = ((), (), s32[]{:S(2)}) async-start(), calls=%async_computation.1 | async-start | bytes 5242880 | tf_op jit(solution)/shard_map/all_gather | solution.py:120
  68.4 4.2 %copy-start.2 = (f32[1024,512]{0,1:T(8,128)}, f32[1024,512]{0,1:T(8,128)S(1)}, u32[]{:S(2)}) copy-start(f32[1024,512]{0,1:T(8,128)S(1)} %copy.81) | copy-start | bytes 6291460
  68.4 1.7 copy-start.8
  163.3 4.6 %copy-start.3 = (f32[1024,512]{0,1:T(8,128)S(1)}, f32[1024,512]{0,1:T(8,128)}, u32[]{:S(2)}) copy-start(f32[1024,512]{0,1:T(8,128)} %copy-done.2) | copy-start | bytes 6291460
  254.3 9.4 %copy-start.1 = (s32[16,2]{0,1:T(2,128)S(1)}, s32[16,2]{0,1:T(2,128)}, u32[]{:S(2)}) copy-start(s32[16,2]{0,1:T(2,128)} %param.12) | copy-start | bytes 388
Sparse Core Ops, SparseCore 0:
  27.1 49.7 all-gather.5
  172.8 46.6 all-gather.3
where the time goes:
time: 274 us; the launch traced here: 271 us
  blocking collectives  106 us (39%)
  local copies, waits for them, and re-layouts  76.8 us (28%)
  matrix products  44 us (16%)
  other arithmetic  19.3 us (7%)
  between operations  13.6 us (5%)
  starting transfers between devices  9.21 us (3%)
    all_to_all x1, blocking collectives, body(): lax.all_to_all(out_weight, 'head', split_axis=1, concat_axis=0, tiled=True)  68.7 us
    dynamic_update_slice x4, local copies, waits for them, and re-layouts, local_attention(): blocks = lax.map(attend_block, jnp.arange(seg_rows // block_rows))  44 us
    all_gather x1, blocking collectives, body(): part_sum = lax.all_gather(feat_sum[None], 'seq', axis=0, tiled=True)  37.5 us
    unnamed x24, local copies, waits for them, and re-layouts  15.5 us
    dot_general x2, matrix products, attend_block(): jnp.einsum('hqk,khd->qhd', weights.astype(jnp.bfloat16), band_values, pre...  12 us
    dot_general x1, matrix products, body(): mixed = jnp.dot(gathered, columns, preferred_element_type=jnp.float32)  9.37 us
    ppermute x2, starting transfers between devices, from_behind(): return lax.ppermute(block, axis, route)  9.17 us
    dot_general x2, matrix products, attend_block(): jnp.einsum('qhd,khd->hqk', query_block, band_keys, preferred_element_type...  8.27 us
  transfers between devices with their start and end apart: 4, of which 0 were waited for; matrix products, arithmetic and copies ran while one was open for 44% of the time, Pallas kernels for 0%

commit v1 on v0

--- a/solution.py
+++ b/solution.py
@@ -118,7 +118,12 @@
         .reshape(seg_rows, head_count * head_width)
     )
     gathered = lax.all_gather(attended, "head", axis=1, tiled=True)
-    columns = lax.all_to_all(out_weight, "head", split_axis=1, concat_axis=0, tiled=True)
+    columns = jnp.concatenate(
+        lax.all_to_all(
+            jnp.stack(jnp.split(out_weight, lax.axis_size("head"), axis=1)), "head", 0, 0
+        ),
+        axis=0,
+    )
     mixed = jnp.dot(gathered, columns, preferred_element_type=jnp.float32)
     return mixed.astype(jnp.bfloat16)
 

time: 274 us -> 265 us (0.967)
  local copies, waits for them, and re-layouts: 76.8 us -> 66.8 us
  blocking collectives: 106 us -> 110 us
    all_to_all x1 -> x0, local copies, waits for them, and re-layouts: 6.34 us -> none  [body(): lax.all_to_all(out_weight, 'head', split_axis=1, concat_axis=0, tiled=True)]
    unnamed x24 -> x23, local copies, waits for them, and re-layouts: 15.5 us -> 9.2 us
    all_to_all x1, blocking collectives: 68.7 us -> 72.1 us  [body(): lax.all_to_all(jnp.stack(jnp.split(out_weight, lax.axis_size('head'), axi...]
  transfers between devices with their start and end apart: 4 -> 4, of which waited for: 0 -> 0; matrix products, arithmetic and copies ran while one was open for 44% -> 41% of each run, Pallas kernels for 0% -> 0%
where the time goes in v1:
time: 265 us; the launch traced here: 262 us
  blocking collectives  110 us (42%)
  local copies, waits for them, and re-layouts  66.8 us (25%)
  matrix products  41.7 us (16%)
  other arithmetic  19.8 us (7%)
  between operations  13.6 us (5%)
  starting transfers between devices  9.21 us (3%)
    all_to_all x1, blocking collectives, body(): lax.all_to_all(jnp.stack(jnp.split(out_weight, lax.axis_size('head'), axi...  72.1 us
    dynamic_update_slice x4, local copies, waits for them, and re-layouts, local_attention(): blocks = lax.map(attend_block, jnp.arange(seg_rows // block_rows))  44 us
    all_gather x1, blocking collectives, body(): part_sum = lax.all_gather(feat_sum[None], 'seq', axis=0, tiled=True)  37.5 us
    dot_general x2, matrix products, attend_block(): jnp.einsum('hqk,khd->qhd', weights.astype(jnp.bfloat16), band_values, pre...  9.72 us
    dot_general x1, matrix products, body(): mixed = jnp.dot(gathered, columns, preferred_element_type=jnp.float32)  9.37 us
    unnamed x23, local copies, waits for them, and re-layouts  9.2 us
    ppermute x2, starting transfers between devices, from_behind(): return lax.ppermute(block, axis, route)  9.17 us
    dot_general x2, matrix products, attend_block(): jnp.einsum('qhd,khd->hqk', query_block, band_keys, preferred_element_type...  8.27 us
  transfers between devices with their start and end apart: 4, of which 0 were waited for; matrix products, arithmetic and copies ran while one was open for 41% of the time, Pallas kernels for 0%

profile of v1, /device:TPU:0, one launch (start us, length us, event | category | flops | bytes accessed | tf_op | source)
XLA Modules:
  0.0 262.2 jit_solution(17488332635209979934)
XLA Ops:
  6.5 0.0 copy-start
  6.5 0.0 all-gather.6.cloned.1.call-start
  6.5 1.6 copy.40
  8.1 0.0 copy-start.4
  8.1 0.9 slice.16
  9.0 0.2 copy-done.4
  9.3 5.7 %collective-permute-start = (bf16[512,512]{0,1:T(8,128)(2,1)}, bf16[512,512]{0,1:T(8,128)(2,1)}, u32[]{:S(2)}, u32[]{:S(2)}) collective-permute-start(bf16[512,512]{0,1:T(8,128)(2,1)} %slice.16), channel_id=1, source_target_pairs={{0,4},{4,8},{8,12},{12,16},{16,20},{20,24},{24,28},{1,5},{5,9},{9,... | collective-permute-start | bytes 1572872 | tf_op jit(solution)/shard_map/ppermute | solution.py:15
  15.0 0.5 copy.42
  15.5 0.8 slice.17
  16.4 3.5 %collective-permute-start.1 = (bf16[512,512]{0,1:T(8,128)(2,1)}, bf16[512,512]{0,1:T(8,128)(2,1)}, u32[]{:S(2)}, u32[]{:S(2)}) collective-permute-start(bf16[512,512]{0,1:T(8,128)(2,1)} %slice.17), channel_id=1, source_target_pairs={{0,4},{4,8},{8,12},{12,16},{16,20},{20,24},{24,28},{1,5},{5,9},{9,... | collective-permute-start | bytes 1572872 | tf_op jit(solution)/shard_map/ppermute | solution.py:15
  19.8 1.8 fusion.35
  21.6 1.8 copy.57
  23.4 3.8 %fusion.29 = f32[4,128,128]{2,1,0:T(8,128)} fusion(f32[1024,4,128]{0,2,1:T(8,128)} %bitcast.91, bf16[1024,512]{1,0:T(8,128)(2,1)} %param.11), kind=kOutput, calls=%fused_computation.43 | convolution fusion | flops 805306368 | bytes 3407872 | tf_op jit(solution)/shard_map/thd,the->hde/dot_general | solution.py:75
  27.2 0.0 all-gather.6.cloned.1.call-update
  27.2 0.0 all-gather.4.cloned.1.call-start
  27.3 0.1 constant_dynamic-slice_fusion
  27.4 37.5 %all_gather.10 = f32[8,4,128]{2,1,0:T(4,128)S(1)} all-gather(f32[1,4,128]{2,1,0:T(4,128)S(1)} %bitcast.101), channel_id=1, replica_groups=mesh['seq'=8,'head'=4] {'seq'}, dimensions={0}, use_global_device_ids=true | all-gather | bytes 18432 | tf_op jit(solution)/shard_map/all_gather | solution.py:82
  64.9 0.0 copy-done.5
  64.9 1.8 fusion.22
  66.7 1.9 copy.63
  68.6 0.0 copy-start.2
  68.6 0.0 copy-start.9
  68.6 0.2 reduce_window_sum.11
  68.8 0.2 dynamic-slice_reduce_fusion
  69.0 0.1 exponential_select_fusion
  69.1 0.2 convolution_bitcast_fusion
  69.3 1.1 fusion.36
  70.4 0.0 copy-done.9
  70.4 0.1 fusion.34
  70.5 2.3 copy.39
  72.8 0.0 collective-permute-done
  72.8 2.6 %pad_maximum_fusion.1 = bf16[1536,512]{0,1:T(8,128)(2,1)} fusion(bf16[1024,512]{0,1:T(8,128)(2,1)} %copy-done.4, bf16[512,512]{0,1:T(8,128)(2,1)} %collective-permute-done), kind=kLoop, calls=%fused_computation.40 | loop fusion | flops 3145728 | bytes 3145728 | tf_op jit(solution)/shard_map/concatenate | solution.py:104
  75.5 1.9 copy.45
  77.4 0.0 collective-permute-done.1
  77.4 2.3 pad_maximum_fusion.2
  79.7 2.6 copy.46
  82.3 74.9 %while.14 = (s32[]{:T(128)}, f32[2,512,4,128]{1,0,3,2:T(2,128)}, s32[2]{0:T(128)S(1)}, s32[1024]{0:T(1024)S(1)}, s32[1536]{0:T(1024)S(1)}, /*index=5*/bf16[1024,...) while((s32[]{:T(128)}, f32[2,512,4,128]{1,0,3,2:T(2,128)}, ...), condition=%wide.region_6.7_spmd.clone.clone, body=%wide.region_3.6_spmd.clone.clone.sunk | while | flops 1650986496 | bytes 56176868 | solution.py:60
  82.3 0.6 dynamic_slice.46
  83.6 0.1 broadcast_compare_fusion.2
  83.7 1.4 and_or_fusion.2
  85.1 4.1 %fusion.57 = (f32[4,512]{1,0:T(4,128)S(1)}, f32[4,512,1536]{2,1,0:T(8,128)S(1)}) fusion(pred[512,1536]{1,0:T(8,128)(4,1)S(1)} %and_or_fusion.2, bf16[1536,4,128]{2,0,1:T(8,128)(2,1)S(1)} %get-tuple-element.340, bf16[1024,4,128]{0,2,1:T(8,128)(2,1)} %get-tuple-element.339, s32[]{:T(128)S(6)} %select_n.64), kind=kOutput, calls=%fused_computation.4.clone.1 | convolution fusion | flops 814741504 | bytes 15474692 | tf_op jit(solution)/shard_map/while/body/eval_jaxpr/qhd,khd->hqk/dot_general | solution.py:38
  89.3 0.0 copy-start.7
  89.3 3.6 %fusion.58 = f32[4,512]{1,0:T(4,128)S(1)} fusion(f32[4,512,1536]{2,1,0:T(8,128)S(1)} %get-tuple-element.306, f32[4,512]{1,0:T(4,128)S(1)} %get-tuple-element.307, pred[512,1536]{1,0:T(8,128)(4,1)S(1)} %and_or_fusion.2), kind=kLoop, calls=%fused_computation.5.clone.1 | loop fusion | flops 12580864 | bytes 13385728 | tf_op jit(solution)/shard_map/while/body/eval_jaxpr/reduce_sum | solution.py:51
  92.9 4.9 %divide_bitcast_fusion.2 = f32[1,512,4,128]{3,1,2,0:T(8,128)} fusion(bf16[1536,4,128]{2,0,1:T(8,128)(2,1)S(1)} %copy-done.7, f32[4,512,1536]{2,1,0:T(8,128)S(1)} %get-tuple-element.306, f32[4,512]{1,0:T(4,128)S(1)} %get-tuple-element.307, pred[512,1536]{1,0:T(8,128)(4,1)S(1)} %and_or_fusion.2, f32[512,4]{0,1:T(4,128)S(1)} %bitcast.98), kind=kOutput, calls=%fused_computation.11.clone.1 | convolution fusion | flops 818151424 | bytes 16007168 | tf_op jit(solution)/shard_map/while/body/eval_jaxpr/hqk,khd->qhd/dot_general | solution.py:52
  97.8 2.4 copy.75
  100.2 19.6 %dynamic_update_slice.10 = f32[2,512,4,128]{1,0,3,2:T(2,128)} dynamic-update-slice(f32[2,512,4,128]{1,0,3,2:T(2,128)} %get-tuple-element.322, f32[1,512,4,128]{1,0,3,2:T(1,128)S(1)} %copy.75, s32[]{:T(128)} %get-tuple-element.321, s32[]{:T(128)} %constant.90.clone.1..sunk, s32[]{:T(128)} %constant.90.clone.1..sunk, s32[]{:T(128)} %constant.90.clone.1..sunk) | dynamic-update-slice | bytes 2097156 | tf_op jit(solution)/shard_map/while/body/jit(dynamic_update_index_in_dim)/dynamic_update_slice | solution.py:60
  119.8 0.6 dynamic_slice.46
  121.0 0.1 broadcast_compare_fusion.2
  121.2 1.4 and_or_fusion.2
  122.6 4.1 %fusion.57 = (f32[4,512]{1,0:T(4,128)S(1)}, f32[4,512,1536]{2,1,0:T(8,128)S(1)}) fusion(pred[512,1536]{1,0:T(8,128)(4,1)S(1)} %and_or_fusion.2, bf16[1536,4,128]{2,0,1:T(8,128)(2,1)S(1)} %get-tuple-element.340, bf16[1024,4,128]{0,2,1:T(8,128)(2,1)} %get-tuple-element.339, s32[]{:T(128)S(6)} %select_n.64), kind=kOutput, calls=%fused_computation.4.clone.1 | convolution fusion | flops 814741504 | bytes 15474692 | tf_op jit(solution)/shard_map/while/body/eval_jaxpr/qhd,khd->hqk/dot_general | solution.py:38
  126.7 3.6 %fusion.58 = f32[4,512]{1,0:T(4,128)S(1)} fusion(f32[4,512,1536]{2,1,0:T(8,128)S(1)} %get-tuple-element.306, f32[4,512]{1,0:T(4,128)S(1)} %get-tuple-element.307, pred[512,1536]{1,0:T(8,128)(4,1)S(1)} %and_or_fusion.2), kind=kLoop, calls=%fused_computation.5.clone.1 | loop fusion | flops 12580864 | bytes 13385728 | tf_op jit(solution)/shard_map/while/body/eval_jaxpr/reduce_sum | solution.py:51
  130.4 4.9 %divide_bitcast_fusion.2 = f32[1,512,4,128]{3,1,2,0:T(8,128)} fusion(bf16[1536,4,128]{2,0,1:T(8,128)(2,1)S(1)} %copy-done.7, f32[4,512,1536]{2,1,0:T(8,128)S(1)} %get-tuple-element.306, f32[4,512]{1,0:T(4,128)S(1)} %get-tuple-element.307, pred[512,1536]{1,0:T(8,128)(4,1)S(1)} %and_or_fusion.2, f32[512,4]{0,1:T(4,128)S(1)} %bitcast.98), kind=kOutput, calls=%fused_computation.11.clone.1 | convolution fusion | flops 818151424 | bytes 16007168 | tf_op jit(solution)/shard_map/while/body/eval_jaxpr/hqk,khd->qhd/dot_general | solution.py:52
  135.3 2.4 copy.75
  137.7 19.6 %dynamic_update_slice.10 = f32[2,512,4,128]{1,0,3,2:T(2,128)} dynamic-update-slice(f32[2,512,4,128]{1,0,3,2:T(2,128)} %get-tuple-element.322, f32[1,512,4,128]{1,0,3,2:T(1,128)S(1)} %copy.75, s32[]{:T(128)} %get-tuple-element.321, s32[]{:T(128)} %constant.90.clone.1..sunk, s32[]{:T(128)} %constant.90.clone.1..sunk, s32[]{:T(128)} %constant.90.clone.1..sunk) | dynamic-update-slice | bytes 2097156 | tf_op jit(solution)/shard_map/while/body/jit(dynamic_update_index_in_dim)/dynamic_update_slice | solution.py:60
  157.3 4.0 %reshape.179 = f32[1024,4,128]{0,2,1:T(8,128)} reshape(f32[2,512,4,128]{1,0,3,2:T(2,128)} %get-tuple-element.133) | data formatting | bytes 4194304 | tf_op jit(solution)/shard_map/reshape | solution.py:61
  161.3 4.6 %fusion.27 = f32[4,1,128,128]{3,1,2,0:T(1,128)S(1)} fusion(f32[8,4,1,1]{0,2,3,1:T(1,128)S(1)} %bitcast.100, f32[8,4,128,128]{3,2,1,0:T(8,128)} %bitcast.95), kind=kOutput, calls=%fused_computation.37 | convolution fusion | flops 6291456 | bytes 2359424 | tf_op jit(solution)/shard_map/nh,nhde->hde/dot_general | solution.py:90
  165.9 0.0 copy-done.3
  165.9 4.8 %fusion.26 = bf16[1024,4,128]{0,2,1:T(8,128)(2,1)} fusion(f32[1024,4,128]{0,2,1:T(8,128)} %reshape.179, f32[4,128,128]{2,1,0:T(8,128)S(1)} %bitcast.97, f32[1024,4,128]{0,2,1:T(8,128)S(1)} %bitcast.90, f32[4]{0:T(128)S(1)} %get-tuple-element.227, f32[1024,4]{0,1:T(4,128)S(1)} %fusion.32, f32[4]{0:T(128)S(1)} %get-tuple-element.228), kind=kOutput, calls=%fused_computation.36 | convolution fusion | flops 807927808 | bytes 5521440 | tf_op jit(solution)/shard_map/thd,hde->the/dot_general | solution.py:93
  170.6 0.0 all-gather.4.cloned.1.call-update
  170.7 2.6 %slice_bitcast_fusion.3 = (bf16[1,512,1024]{2,1,0:T(8,128)(2,1)S(1)}, bf16[1,512,1024]{2,1,0:T(8,128)(2,1)S(1)}, bf16[1,512,1024]{2,1,0:T(8,128)(2,1)S(1)}, bf16[1,512,1024]{2,1,0:T(8,128)(2,1)S(1)}) fusion(bf16[512,4096]{1,0:T(8,128)(2,1)} %param.15), kind=kLoop, calls=%fused_computation.49 | loop fusion | bytes 8388608 | tf_op jit(solution)/shard_map/stack | solution.py:123
  173.3 0.6 pad_maximum_fusion
  173.9 72.1 %all_to_all.5 = bf16[4,512,1024]{2,1,0:T(8,128)(2,1)} all-to-all(bf16[4,512,1024]{2,1,0:T(8,128)(2,1)S(1)} %pad_maximum_fusion), channel_id=1, replica_groups=mesh['seq'=8,'head'=4] {'head'}, dimensions={0} | all-to-all | bytes 8388608 | tf_op jit(solution)/shard_map/all_to_all | solution.py:122
  246.0 9.4 %convolution_convert_fusion = bf16[1024,1024]{1,0:T(8,128)(2,1)} fusion(bf16[1024,2048]{0,1:T(8,128)(2,1)} %all-gather.4.cloned.1.call-done, bf16[2048,1024]{1,0:T(8,128)(2,1)} %bitcast.94), kind=kOutput, calls=%fused_computation.39 | convolution fusion | flops 4296015872 | bytes 10485760 | tf_op jit(solution)/shard_map/dot_general | solution.py:127
  255.4 0.0 copy-done.1
  (30 shorter events, 0.1 us)
Async XLA Ops:
  6.5 20.7 %copy-start = (s32[16,2]{0,1:T(2,128)S(1)}, s32[16,2]{0,1:T(2,128)}, u32[]{:S(2)}) copy-start(s32[16,2]{0,1:T(2,128)} %param.12) | copy-start | bytes 388
  6.5 8.4 %copy-start.6 = (bf16[1024,512]{1,0:T(8,128)(2,1)S(1)}, bf16[1024,512]{1,0:T(8,128)(2,1)}, u32[]{:S(2)}) copy-start(bf16[1024,512]{1,0:T(8,128)(2,1)} %param.11) | copy-start | bytes 3145732
  6.5 154.8 %all-gather.6.cloned.1.call-start = ((), (), s32[]{:S(2)}) async-start(), calls=%async_computation.2 | async-start | bytes 2359296 | tf_op jit(solution)/shard_map/all_gather | solution.py:81
  8.1 1.1 copy-start.4
  9.3 63.6 %collective-permute-start = (bf16[512,512]{0,1:T(8,128)(2,1)}, bf16[512,512]{0,1:T(8,128)(2,1)}, u32[]{:S(2)}, u32[]{:S(2)}) collective-permute-start(bf16[512,512]{0,1:T(8,128)(2,1)} %slice.16), channel_id=1, source_target_pairs={{0,4},{4,8},{8,12},{12,16},{16,20},{20,24},{24,28},{1,5},{5,9},{9,... | collective-permute-start | bytes 1572872 | tf_op jit(solution)/shard_map/ppermute | solution.py:15
  16.4 61.0 %collective-permute-start.1 = (bf16[512,512]{0,1:T(8,128)(2,1)}, bf16[512,512]{0,1:T(8,128)(2,1)}, u32[]{:S(2)}, u32[]{:S(2)}) collective-permute-start(bf16[512,512]{0,1:T(8,128)(2,1)} %slice.17), channel_id=1, source_target_pairs={{0,4},{4,8},{8,12},{12,16},{16,20},{20,24},{24,28},{1,5},{5,9},{9,... | collective-permute-start | bytes 1572872 | tf_op jit(solution)/shard_map/ppermute | solution.py:15
  23.4 4.0 %copy-start.8 = (f32[8,4]{0,1:T(4,128)S(1)}, f32[8,4]{0,1:T(4,128)}, u32[]{:S(2)}) copy-start(f32[8,4]{0,1:T(4,128)} %param.13) | copy-start | bytes 388
  23.4 41.5 %copy-start.5 = (bf16[1024,512]{1,0:T(8,128)(2,1)S(1)}, bf16[1024,512]{1,0:T(8,128)(2,1)}, u32[]{:S(2)}) copy-start(bf16[1024,512]{1,0:T(8,128)(2,1)} %param.9) | copy-start | bytes 3145732
  27.2 218.8 %all-gather.4.cloned.1.call-start = ((), (), s32[]{:S(2)}) async-start(), calls=%async_computation.1 | async-start | bytes 5242880 | tf_op jit(solution)/shard_map/all_gather | solution.py:120
  68.6 4.2 %copy-start.2 = (f32[1024,512]{0,1:T(8,128)}, f32[1024,512]{0,1:T(8,128)S(1)}, u32[]{:S(2)}) copy-start(f32[1024,512]{0,1:T(8,128)S(1)} %copy.63) | copy-start | bytes 6291460
  68.6 1.7 copy-start.9
  89.3 3.7 %copy-start.7 = (bf16[1536,4,128]{2,0,1:T(8,128)(2,1)S(1)}, bf16[1536,4,128]{2,0,1:T(8,128)(2,1)}, u32[]{:S(2)}) copy-start(bf16[1536,4,128]{2,0,1:T(8,128)(2,1)} %get-tuple-element.341) | copy-start | bytes 4718596 | tf_op jit(solution)/shard_map/while
  126.7 3.7 %copy-start.7 = (bf16[1536,4,128]{2,0,1:T(8,128)(2,1)S(1)}, bf16[1536,4,128]{2,0,1:T(8,128)(2,1)}, u32[]{:S(2)}) copy-start(bf16[1536,4,128]{2,0,1:T(8,128)(2,1)} %get-tuple-element.341) | copy-start | bytes 4718596 | tf_op jit(solution)/shard_map/while
  161.3 4.6 %copy-start.3 = (f32[1024,512]{0,1:T(8,128)S(1)}, f32[1024,512]{0,1:T(8,128)}, u32[]{:S(2)}) copy-start(f32[1024,512]{0,1:T(8,128)} %copy-done.2) | copy-start | bytes 6291460
  246.0 9.4 %copy-start.1 = (s32[16,2]{0,1:T(2,128)S(1)}, s32[16,2]{0,1:T(2,128)}, u32[]{:S(2)}) copy-start(s32[16,2]{0,1:T(2,128)} %param.12) | copy-start | bytes 388
Sparse Core Ops, SparseCore 0:
  27.3 49.7 all-gather.5
  170.8 52.3 all-gather.3
